TPU v7x, 256 devices: a whole 4x4x8 slice. The times are simulated.
256 devices in a mesh: heads: 4 (over y_hi, core), blk: 64 (over y_lo, z, x).
Axes of the slice: x: 4, y: 4 (y_hi: 2, y_lo: 2; y = y_hi * 2 + y_lo), z: 8, core: 2. Of those that a mesh axis runs over, the one named last changes fastest.
Arguments:
- tokens: bfloat16 [32768, 4096], P(('blk', 'heads')), may hold values from -6 to 6
- w_query: bfloat16 [4096, 2048], P('blk', 'heads'), may hold values from -0.75 to 0.75
- key_value_weight: bfloat16 [4096, 2, 512], P('blk', None, 'heads'), may hold values from -0.75 to 0.75
- w_out: bfloat16 [2048, 4096], P(('heads', 'blk')), may hold values from -0.5 to 0.5
- doc_lengths: int32 [16], replicated, may hold values from 1 to 8192, 32768 in all
Outputs:
- attended: bfloat16 [32768, 4096], P(('blk', 'heads'))
Inputs may be any that keep to these rules, and one draw needn't show every extreme that they name: `doc_lengths`: the 16 lengths sum to 32768; the longest document has exactly 8192 tokens.
All inputs are finite; a program needn't handle non-finite values.
Results may differ from a plain program's by a relative error of at most 0.012.
Values may be sent and summed in bfloat16 or wider, within the bound.
A program may use at most 128 MiB of HBM per device.

v0:
```python
import jax
import jax.numpy as jnp
from jax import lax
from jax.sharding import PartitionSpec as P

HEAD_SIZE = 128
norm_epsilon = 1e-05
rope_base = 500000.0
masked_score = -1e30


def in_one_piece(arrays, axis, dim, along):
    columns = [a.reshape(*a.shape[:along], -1) for a in arrays]
    both = jnp.concatenate(columns, axis=along)
    whole, at, finished = (lax.all_gather(both, axis, axis=dim, tiled=True), 0, [])
    for a, column in zip(arrays, columns):
        piece = whole[..., at : at + column.shape[along]]
        finished.append(piece.reshape(*piece.shape[:along], *a.shape[along:]))
        at += column.shape[along]
    return tuple(finished)


def shifted(value, axis, steps):
    count = lax.axis_size(axis)
    first, last = (max(0, -steps), min(count, count - steps))
    return lax.ppermute(value, axis, [(source, source + steps) for source in range(first, last)])


def locate_documents(positions, doc_lengths):
    ends = jnp.cumsum(doc_lengths)
    after = positions[:, None] >= ends[None, :]
    ident = jnp.sum(after.astype(jnp.int32), axis=1)
    starts = jnp.sum(jnp.where(after, doc_lengths[None, :], 0), axis=1)
    return (ident, starts)


def apply_rotation(values, relative_offset):
    half = values.shape[-1] // 2
    freqs = jnp.power(rope_base, -2.0 * jnp.arange(half, dtype=jnp.float32) / values.shape[-1])
    angle = relative_offset.astype(jnp.float32)[:, None] * freqs[None, :]
    cosine = jnp.cos(angle)[:, None, :]
    sine = jnp.sin(angle)[:, None, :]
    first = values[..., :half]
    second = values[..., half:]
    return jnp.concatenate(
        [first * cosine - second * sine, second * cosine + first * sine], axis=-1
    )


def on_device(tokens, w_query, key_value_weight, w_out, doc_lengths):
    blk_index = lax.axis_index("blk")
    reach = lax.axis_size("blk") // 4
    values = tokens.astype(jnp.float32)
    normalized_input = (
        values * lax.rsqrt(jnp.mean(values * values, axis=1, keepdims=True) + norm_epsilon)
    ).astype(jnp.bfloat16)
    block_input = lax.all_gather(normalized_input, "heads", axis=0, tiled=True)
    block_rows = block_input.shape[0]
    query_cols = w_query.shape[1]
    kv_cols = key_value_weight.shape[2]
    pieces = in_one_piece((w_query, key_value_weight), "blk", 0, 1)
    count = pieces[0].shape[0]
    query_part = jnp.dot(block_input, pieces[0], preferred_element_type=jnp.float32)
    keyval_part = jnp.dot(
        block_input, pieces[1].reshape(count, 2 * kv_cols), preferred_element_type=jnp.float32
    )
    positions = blk_index * block_rows + jnp.arange(block_rows, dtype=jnp.int32)
    ident, starts = locate_documents(positions, doc_lengths)
    relative_offset = positions - starts
    query_heads = query_cols // HEAD_SIZE
    kv_heads = kv_cols // HEAD_SIZE
    head_group = query_heads // kv_heads
    query_rows = apply_rotation(
        query_part.reshape(block_rows, query_heads, HEAD_SIZE), relative_offset
    ).astype(jnp.bfloat16)
    query_rows = query_rows.reshape(block_rows, kv_heads, head_group, HEAD_SIZE)
    rotated_keys = apply_rotation(
        keyval_part[:, :kv_cols].reshape(block_rows, kv_heads, HEAD_SIZE), relative_offset
    ).astype(jnp.bfloat16)
    value_rows = (
        keyval_part[:, kv_cols:].reshape(block_rows, kv_heads, HEAD_SIZE).astype(jnp.bfloat16)
    )
    kv_block = jnp.stack([rotated_keys, value_rows], axis=1)
    scale = HEAD_SIZE ** (-0.5)

    def attend_tile(state, kv_now, distance):
        key_pos = (blk_index - distance) * block_rows + jnp.arange(block_rows, dtype=jnp.int32)
        key_doc, unused_k = locate_documents(key_pos, doc_lengths)
        keep = (
            (key_pos[None, :] >= 0)
            & (key_pos[None, :] <= positions[:, None])
            & (key_doc[None, :] == ident[:, None])
        )
        highest, totals, accum = state
        scores = (
            jnp.einsum(
                "qhgd,khd->hgqk", query_rows, kv_now[:, 0], preferred_element_type=jnp.float32
            )
            * scale
        )
        scores = jnp.where(keep, scores, masked_score)
        new_high = jnp.maximum(highest, jnp.max(scores, axis=-1))
        fading = jnp.exp(highest - new_high)
        probs = jnp.where(keep, jnp.exp(scores - new_high[..., None]), 0.0)
        totals = totals * fading + jnp.sum(probs, axis=-1)
        update = jnp.einsum(
            "hgqk,khd->hgqd",
            probs.astype(jnp.bfloat16),
            kv_now[:, 1],
            preferred_element_type=jnp.float32,
        )
        accum = accum * fading[..., None] + update
        return (new_high, totals, accum)

    initial = (
        jnp.full((kv_heads, head_group, block_rows), masked_score, jnp.float32),
        jnp.zeros((kv_heads, head_group, block_rows), jnp.float32),
        jnp.zeros((kv_heads, head_group, block_rows, HEAD_SIZE), jnp.float32),
    )
    state = attend_tile(initial, kv_block, 0)

    def advance(distance, carry):
        kv_now, inner = carry
        kv_now = shifted(kv_now, "blk", 1)
        return (kv_now, attend_tile(inner, kv_now, distance))

    unused_kv, state = lax.fori_loop(1, reach + 1, advance, (kv_block, state))
    highest, totals, accum = state
    mixed = accum / totals[..., None]
    mixed = mixed.transpose(2, 0, 1, 3).reshape(block_rows, query_cols).astype(jnp.bfloat16)
    head_rows = lax.all_gather(w_out, "blk", axis=0, tiled=True)
    return lax.psum_scatter(
        jnp.dot(mixed, head_rows, preferred_element_type=jnp.float32).astype(jnp.bfloat16),
        "heads",
        scatter_dimension=0,
        tiled=True,
    )


def solution(mesh):
    return jax.shard_map(
        on_device,
        mesh=mesh,
        in_specs=(
            P(("blk", "heads"), None),
            P("blk", "heads"),
            P("blk", None, "heads"),
            P(("heads", "blk"), None),
            P(),
        ),
        out_specs=P(("blk", "heads"), None),
        check_vma=False,
    )
```

profile of v0, /device:TPU:1, one launch (start us, length us, event | category | flops | bytes accessed | tf_op | source)
XLA Modules:
  0.0 733.6 jit_solution(8738411729264827400)
XLA Ops:
  8.1 2.5 fusion.27
  13.8 42.2 %all-gather.4.cloned.1.call-done = bf16[512,4096]{1,0:T(8,128)(2,1)} async-done(((bf16[128,4096]{1,0:T(8,128)(2,1)}), bf16[512,4096]{1,0:T(8,128)(2,1)}) %all-gather.4.cloned.1.call-update) | async-done | bytes 4194320 | tf_op jit(solution)/shard_map/all_gather | solution.py:57
  56.0 262.9 %all-gather.6.cloned.1.call-done = bf16[4096,768]{1,0:T(8,128)(2,1)} async-done(((bf16[64,768]{1,0:T(8,128)(2,1)}), bf16[4096,768]{1,0:T(8,128)(2,1)}) %all-gather.6.cloned.1.call-update) | async-done | bytes 6291472 | tf_op jit(solution)/shard_map/all_gather | solution.py:15
  318.9 4.2 fusion.29
  324.8 5.8 fusion.21
  335.9 211.9 %while.22 = (s32[]{:T(128)}, bf16[512,2,1,128]{3,0,2,1:T(8,128)(2,1)S(1)}, f32[1,4,512]{2,1,0:T(4,128)S(1)}, f32[1,4,512]{2,1,0:T(4,128)S(1)}, f32[1,4,512,128]{...) while((s32[]{:T(128)}, ...), condition=%wide.region_10.11_spmd.clone, body=%wide.region_6.10_spmd.clone.sunk | while | flops 552107520 | bytes 18236672 | solution.py:127
  336.1 2.2 collective-permute-start
  338.8 2.9 collective-permute-done
  343.7 1.9 fusion.78
  345.7 4.2 collective-permute-start
  350.3 2.9 collective-permute-done
  357.2 3.8 collective-permute-start
  361.5 2.8 collective-permute-done
  366.3 1.9 fusion.78
  368.3 3.8 collective-permute-start
  372.6 3.5 collective-permute-done
  378.1 1.9 fusion.78
  380.0 4.0 collective-permute-start
  384.4 6.1 collective-permute-done
  392.5 1.9 fusion.78
  394.4 3.8 collective-permute-start
  398.7 6.4 collective-permute-done
  407.1 1.9 fusion.78
  409.0 4.2 collective-permute-start
  413.7 5.8 collective-permute-done
  421.5 1.9 fusion.78
  423.4 4.2 collective-permute-start
  428.1 4.2 collective-permute-done
  436.3 4.3 collective-permute-start
  441.1 4.3 collective-permute-done
  449.3 5.2 collective-permute-start
  455.0 4.1 collective-permute-done
  461.1 1.9 fusion.78
  463.0 5.1 collective-permute-start
  468.6 3.3 collective-permute-done
  475.8 4.7 collective-permute-start
  481.0 2.8 collective-permute-done
  487.7 11.1 %collective-permute-start = (bf16[512,2,1,128]{3,0,2,1:T(8,128)(2,1)S(1)}, bf16[512,2,1,128]{3,0,2,1:T(8,128)(2,1)S(1)}, u32[]{:S(2)}, u32[]{:S(2)}) collective-permute-start(bf16[512,2,1,128]{3,0,2,1:T(8,128)(2,1)S(1)} %get-tuple-element.421), channel_id=1, source_target_pairs={{0,1},{1,2},{2,3},{3,4},{4,5},{5,6},{6,7},{7,8},{8,9},{9,10},{10,1... | collective-permute-start | bytes 786440 | tf_op jit(solution)/shard_map/while/body/eval_jaxpr/ppermute | solution.py:26
  499.3 3.7 collective-permute-done
  506.9 5.6 collective-permute-start
  513.0 3.3 collective-permute-done
  520.2 5.8 collective-permute-start
  526.5 3.6 collective-permute-done
  534.1 6.3 collective-permute-start
  540.9 3.0 collective-permute-done
  548.3 70.6 %all-gather.8.cloned.1.call-done = bf16[512,4096]{1,0:T(8,128)(2,1)} async-done(((bf16[8,4096]{1,0:T(8,128)(2,1)}), bf16[512,4096]{1,0:T(8,128)(2,1)}) %all-gather.8.cloned.1.call-update) | async-done | bytes 4194320 | tf_op jit(solution)/shard_map/all_gather | solution.py:131
  618.9 6.5 convolution_convert_fusion
  625.4 101.6 %reduce-scatter.2.cloned.1.call-done = bf16[128,4096]{1,0:T(8,128)(2,1)} async-done(((bf16[512,4096]{1,0:T(8,128)(2,1)}), bf16[128,4096]{1,0:T(8,128)(2,1)}) %reduce-scatter.2.cloned.1.call-update) | async-done | bytes 1048592 | tf_op jit(solution)/shard_map/reduce_scatter | solution.py:132
  (218 shorter events, 67.7 us)
Async XLA Ops:
  6.5 4.1 copy-start.4
  6.5 4.1 copy-start.3
  6.5 5.6 copy-start.5
  6.5 49.5 %all-gather.4.cloned.1.call-start = ((), (), s32[]{:S(2)}) async-start(), calls=%async_computation.1 | async-start | bytes 5242880 | tf_op jit(solution)/shard_map/all_gather | solution.py:57
  10.6 308.3 %all-gather.6.cloned.1.call-start = ((), (), s32[]{:S(2)}) async-start(), calls=%async_computation.2 | async-start | bytes 6389760 | tf_op jit(solution)/shard_map/all_gather | solution.py:15
  11.3 607.6 %all-gather.8.cloned.1.call-start = ((), (), s32[]{:S(2)}) async-start(), calls=%async_computation.3 | async-start | bytes 4259840 | tf_op jit(solution)/shard_map/all_gather | solution.py:131
  12.1 715.0 %reduce-scatter.2.cloned.1.call-start = ((), (), s32[]{:S(2)}) async-start(), calls=%async_computation.4 | async-start | bytes 5242880 | tf_op jit(solution)/shard_map/reduce_scatter | solution.py:132
  323.1 0.8 copy-start
  331.7 2.3 copy-start.1
  334.0 1.9 copy-start.2
  336.1 5.6 collective-permute-start
  345.7 7.6 %collective-permute-start = (bf16[512,2,1,128]{3,0,2,1:T(8,128)(2,1)S(1)}, bf16[512,2,1,128]{3,0,2,1:T(8,128)(2,1)S(1)}, u32[]{:S(2)}, u32[]{:S(2)}) collective-permute-start(bf16[512,2,1,128]{3,0,2,1:T(8,128)(2,1)S(1)} %get-tuple-element.421), channel_id=1, source_target_pairs={{0,1},{1,2},{2,3},{3,4},{4,5},{5,6},{6,7},{7,8},{8,9},{9,10},{10,1... | collective-permute-start | bytes 786440 | tf_op jit(solution)/shard_map/while/body/eval_jaxpr/ppermute | solution.py:26
  357.2 7.1 collective-permute-start
  368.3 7.8 %collective-permute-start = (bf16[512,2,1,128]{3,0,2,1:T(8,128)(2,1)S(1)}, bf16[512,2,1,128]{3,0,2,1:T(8,128)(2,1)S(1)}, u32[]{:S(2)}, u32[]{:S(2)}) collective-permute-start(bf16[512,2,1,128]{3,0,2,1:T(8,128)(2,1)S(1)} %get-tuple-element.421), channel_id=1, source_target_pairs={{0,1},{1,2},{2,3},{3,4},{4,5},{5,6},{6,7},{7,8},{8,9},{9,10},{10,1... | collective-permute-start | bytes 786440 | tf_op jit(solution)/shard_map/while/body/eval_jaxpr/ppermute | solution.py:26
  380.0 10.5 %collective-permute-start = (bf16[512,2,1,128]{3,0,2,1:T(8,128)(2,1)S(1)}, bf16[512,2,1,128]{3,0,2,1:T(8,128)(2,1)S(1)}, u32[]{:S(2)}, u32[]{:S(2)}) collective-permute-start(bf16[512,2,1,128]{3,0,2,1:T(8,128)(2,1)S(1)} %get-tuple-element.421), channel_id=1, source_target_pairs={{0,1},{1,2},{2,3},{3,4},{4,5},{5,6},{6,7},{7,8},{8,9},{9,10},{10,1... | collective-permute-start | bytes 786440 | tf_op jit(solution)/shard_map/while/body/eval_jaxpr/ppermute | solution.py:26
  394.4 10.7 %collective-permute-start = (bf16[512,2,1,128]{3,0,2,1:T(8,128)(2,1)S(1)}, bf16[512,2,1,128]{3,0,2,1:T(8,128)(2,1)S(1)}, u32[]{:S(2)}, u32[]{:S(2)}) collective-permute-start(bf16[512,2,1,128]{3,0,2,1:T(8,128)(2,1)S(1)} %get-tuple-element.421), channel_id=1, source_target_pairs={{0,1},{1,2},{2,3},{3,4},{4,5},{5,6},{6,7},{7,8},{8,9},{9,10},{10,1... | collective-permute-start | bytes 786440 | tf_op jit(solution)/shard_map/while/body/eval_jaxpr/ppermute | solution.py:26
  409.0 10.5 %collective-permute-start = (bf16[512,2,1,128]{3,0,2,1:T(8,128)(2,1)S(1)}, bf16[512,2,1,128]{3,0,2,1:T(8,128)(2,1)S(1)}, u32[]{:S(2)}, u32[]{:S(2)}) collective-permute-start(bf16[512,2,1,128]{3,0,2,1:T(8,128)(2,1)S(1)} %get-tuple-element.421), channel_id=1, source_target_pairs={{0,1},{1,2},{2,3},{3,4},{4,5},{5,6},{6,7},{7,8},{8,9},{9,10},{10,1... | collective-permute-start | bytes 786440 | tf_op jit(solution)/shard_map/while/body/eval_jaxpr/ppermute | solution.py:26
  423.4 8.9 %collective-permute-start = (bf16[512,2,1,128]{3,0,2,1:T(8,128)(2,1)S(1)}, bf16[512,2,1,128]{3,0,2,1:T(8,128)(2,1)S(1)}, u32[]{:S(2)}, u32[]{:S(2)}) collective-permute-start(bf16[512,2,1,128]{3,0,2,1:T(8,128)(2,1)S(1)} %get-tuple-element.421), channel_id=1, source_target_pairs={{0,1},{1,2},{2,3},{3,4},{4,5},{5,6},{6,7},{7,8},{8,9},{9,10},{10,1... | collective-permute-start | bytes 786440 | tf_op jit(solution)/shard_map/while/body/eval_jaxpr/ppermute | solution.py:26
  436.3 9.1 %collective-permute-start = (bf16[512,2,1,128]{3,0,2,1:T(8,128)(2,1)S(1)}, bf16[512,2,1,128]{3,0,2,1:T(8,128)(2,1)S(1)}, u32[]{:S(2)}, u32[]{:S(2)}) collective-permute-start(bf16[512,2,1,128]{3,0,2,1:T(8,128)(2,1)S(1)} %get-tuple-element.421), channel_id=1, source_target_pairs={{0,1},{1,2},{2,3},{3,4},{4,5},{5,6},{6,7},{7,8},{8,9},{9,10},{10,1... | collective-permute-start | bytes 786440 | tf_op jit(solution)/shard_map/while/body/eval_jaxpr/ppermute | solution.py:26
  449.3 9.8 %collective-permute-start = (bf16[512,2,1,128]{3,0,2,1:T(8,128)(2,1)S(1)}, bf16[512,2,1,128]{3,0,2,1:T(8,128)(2,1)S(1)}, u32[]{:S(2)}, u32[]{:S(2)}) collective-permute-start(bf16[512,2,1,128]{3,0,2,1:T(8,128)(2,1)S(1)} %get-tuple-element.421), channel_id=1, source_target_pairs={{0,1},{1,2},{2,3},{3,4},{4,5},{5,6},{6,7},{7,8},{8,9},{9,10},{10,1... | collective-permute-start | bytes 786440 | tf_op jit(solution)/shard_map/while/body/eval_jaxpr/ppermute | solution.py:26
  463.0 8.8 %collective-permute-start = (bf16[512,2,1,128]{3,0,2,1:T(8,128)(2,1)S(1)}, bf16[512,2,1,128]{3,0,2,1:T(8,128)(2,1)S(1)}, u32[]{:S(2)}, u32[]{:S(2)}) collective-permute-start(bf16[512,2,1,128]{3,0,2,1:T(8,128)(2,1)S(1)} %get-tuple-element.421), channel_id=1, source_target_pairs={{0,1},{1,2},{2,3},{3,4},{4,5},{5,6},{6,7},{7,8},{8,9},{9,10},{10,1... | collective-permute-start | bytes 786440 | tf_op jit(solution)/shard_map/while/body/eval_jaxpr/ppermute | solution.py:26
  475.8 8.0 %collective-permute-start = (bf16[512,2,1,128]{3,0,2,1:T(8,128)(2,1)S(1)}, bf16[512,2,1,128]{3,0,2,1:T(8,128)(2,1)S(1)}, u32[]{:S(2)}, u32[]{:S(2)}) collective-permute-start(bf16[512,2,1,128]{3,0,2,1:T(8,128)(2,1)S(1)} %get-tuple-element.421), channel_id=1, source_target_pairs={{0,1},{1,2},{2,3},{3,4},{4,5},{5,6},{6,7},{7,8},{8,9},{9,10},{10,1... | collective-permute-start | bytes 786440 | tf_op jit(solution)/shard_map/while/body/eval_jaxpr/ppermute | solution.py:26
  487.7 15.3 %collective-permute-start = (bf16[512,2,1,128]{3,0,2,1:T(8,128)(2,1)S(1)}, bf16[512,2,1,128]{3,0,2,1:T(8,128)(2,1)S(1)}, u32[]{:S(2)}, u32[]{:S(2)}) collective-permute-start(bf16[512,2,1,128]{3,0,2,1:T(8,128)(2,1)S(1)} %get-tuple-element.421), channel_id=1, source_target_pairs={{0,1},{1,2},{2,3},{3,4},{4,5},{5,6},{6,7},{7,8},{8,9},{9,10},{10,1... | collective-permute-start | bytes 786440 | tf_op jit(solution)/shard_map/while/body/eval_jaxpr/ppermute | solution.py:26
  506.9 9.4 %collective-permute-start = (bf16[512,2,1,128]{3,0,2,1:T(8,128)(2,1)S(1)}, bf16[512,2,1,128]{3,0,2,1:T(8,128)(2,1)S(1)}, u32[]{:S(2)}, u32[]{:S(2)}) collective-permute-start(bf16[512,2,1,128]{3,0,2,1:T(8,128)(2,1)S(1)} %get-tuple-element.421), channel_id=1, source_target_pairs={{0,1},{1,2},{2,3},{3,4},{4,5},{5,6},{6,7},{7,8},{8,9},{9,10},{10,1... | collective-permute-start | bytes 786440 | tf_op jit(solution)/shard_map/while/body/eval_jaxpr/ppermute | solution.py:26
  520.2 9.9 %collective-permute-start = (bf16[512,2,1,128]{3,0,2,1:T(8,128)(2,1)S(1)}, bf16[512,2,1,128]{3,0,2,1:T(8,128)(2,1)S(1)}, u32[]{:S(2)}, u32[]{:S(2)}) collective-permute-start(bf16[512,2,1,128]{3,0,2,1:T(8,128)(2,1)S(1)} %get-tuple-element.421), channel_id=1, source_target_pairs={{0,1},{1,2},{2,3},{3,4},{4,5},{5,6},{6,7},{7,8},{8,9},{9,10},{10,1... | collective-permute-start | bytes 786440 | tf_op jit(solution)/shard_map/while/body/eval_jaxpr/ppermute | solution.py:26
  534.1 9.8 %collective-permute-start = (bf16[512,2,1,128]{3,0,2,1:T(8,128)(2,1)S(1)}, bf16[512,2,1,128]{3,0,2,1:T(8,128)(2,1)S(1)}, u32[]{:S(2)}, u32[]{:S(2)}) collective-permute-start(bf16[512,2,1,128]{3,0,2,1:T(8,128)(2,1)S(1)} %get-tuple-element.421), channel_id=1, source_target_pairs={{0,1},{1,2},{2,3},{3,4},{4,5},{5,6},{6,7},{7,8},{8,9},{9,10},{10,1... | collective-permute-start | bytes 786440 | tf_op jit(solution)/shard_map/while/body/eval_jaxpr/ppermute | solution.py:26
Sparse Core Ops, SparseCore 0:
  10.7 45.2 all-gather.3
  57.8 261.0 all-gather.5
  320.7 298.1 all-gather.7
  625.5 101.4 reduce-scatter.1
where the time goes:
time: 734 us
  waiting for transfers between devices  541 us (74%)
  starting transfers between devices  78.5 us (11%)
  matrix products  63.8 us (9%)
  other arithmetic  32.9 us (4%)
  between operations  13.4 us (2%)
    all_gather x1, waiting for transfers between devices, in_one_piece(): lax.all_gather(both, axis, axis=dim, tiled=True)  263 us
    reduce_scatter x1, waiting for transfers between devices, on_device(): lax.psum_scatter(jnp.dot(mixed, head_rows, preferred_element_type=jnp.flo...  102 us
    ppermute x16, starting transfers between devices, shifted(): lax.ppermute(value, axis, [(source, source + steps) for source in range(f...  78.4 us
    all_gather x1, waiting for transfers between devices, on_device(): head_rows = lax.all_gather(w_out, 'blk', axis=0, tiled=True)  70.6 us
    ppermute x16, waiting for transfers between devices, shifted(): lax.ppermute(value, axis, [(source, source + steps) for source in range(f...  62.8 us
    all_gather x1, waiting for transfers between devices, on_device(): block_input = lax.all_gather(normalized_input, 'heads', axis=0, tiled=True)  42.2 us
    dot_general x17, matrix products, attend_tile(): jnp.einsum('hgqk,khd->hgqd', probs.astype(jnp.bfloat16), kv_now[:, 1], pr...  32.2 us
    reduce_sum x17, other arithmetic, attend_tile(): totals = totals * fading + jnp.sum(probs, axis=-1)  17.7 us
  transfers between devices with their start and end apart: 20, of which 20 were waited for; matrix products, arithmetic and copies ran while one was open for 12% of the time, Pallas kernels for 0%

commit v1 on v0

--- a/solution.py
+++ b/solution.py
@@ -54,7 +54,10 @@
     normalized_input = (
         values * lax.rsqrt(jnp.mean(values * values, axis=1, keepdims=True) + norm_epsilon)
     ).astype(jnp.bfloat16)
-    block_input = lax.all_gather(normalized_input, "heads", axis=0, tiled=True)
+    size = lax.axis_size("heads")
+    blocks = jnp.stack([normalized_input for _ in range(size)])
+    blocks = lax.all_to_all(blocks, "heads", split_axis=0, concat_axis=0)
+    block_input = jnp.concatenate(blocks, axis=0)
     block_rows = block_input.shape[0]
     query_cols = w_query.shape[1]
     kv_cols = key_value_weight.shape[2]

time: 734 us -> 693 us (0.944)
  waiting for transfers between devices: 541 us -> 479 us
  local copies, waits for them, and re-layouts: 2.52 us -> 15.3 us
  starting transfers between devices: 78.5 us -> 87.8 us
    all_gather x1, waiting for transfers between devices: 263 us -> 192 us  [in_one_piece(): lax.all_gather(both, axis, axis=dim, tiled=True)]
    all_to_all x0 -> x1, waiting for transfers between devices: none -> 59.8 us  [on_device(): blocks = lax.all_to_all(blocks, 'heads', split_axis=0, concat_axis=0)]
    all_gather x1 -> x0, waiting for transfers between devices: 42.2 us -> none  [on_device(): block_input = lax.all_gather(normalized_input, 'heads', axis=0, tiled=True)]
    dot_general x0 -> x2, local copies, waits for them, and re-layouts: none -> 10.8 us  [on_device(): jnp.dot(block_input, pieces[0], preferred_element_type=jnp.float32)]
    all_gather x1, waiting for transfers between devices: 70.6 us -> 61.1 us  [on_device(): head_rows = lax.all_gather(w_out, 'blk', axis=0, tiled=True)]
    all_to_all x0 -> x1, starting transfers between devices: none -> 8.13 us  [on_device(): blocks = lax.all_to_all(blocks, 'heads', split_axis=0, concat_axis=0)]
  transfers between devices with their start and end apart: 20 -> 20, of which waited for: 20 -> 20; matrix products, arithmetic and copies ran while one was open for 12% -> 15% of each run, Pallas kernels for 0% -> 0%
where the time goes in v1:
time: 693 us; the launch traced here: 692 us
  waiting for transfers between devices  479 us (69%)
  starting transfers between devices  87.8 us (13%)
  matrix products  63.5 us (9%)
  other arithmetic  32 us (5%)
  local copies, waits for them, and re-layouts  15.3 us (2%)
  between operations  13.3 us (2%)
    all_gather x1, waiting for transfers between devices, in_one_piece(): lax.all_gather(both, axis, axis=dim, tiled=True)  192 us
    reduce_scatter x1, waiting for transfers between devices, on_device(): lax.psum_scatter(jnp.dot(mixed, head_rows, preferred_element_type=jnp.flo...  102 us
    ppermute x16, starting transfers between devices, shifted(): lax.ppermute(value, axis, [(source, source + steps) for source in range(f...  79.6 us
    ppermute x16, waiting for transfers between devices, shifted(): lax.ppermute(value, axis, [(source, source + steps) for source in range(f...  64.2 us
    all_gather x1, waiting for transfers between devices, on_device(): head_rows = lax.all_gather(w_out, 'blk', axis=0, tiled=True)  61.1 us
    all_to_all x1, waiting for transfers between devices, on_device(): blocks = lax.all_to_all(blocks, 'heads', split_axis=0, concat_axis=0)  59.8 us
    dot_general x17, matrix products, attend_tile(): jnp.einsum('hgqk,khd->hgqd', probs.astype(jnp.bfloat16), kv_now[:, 1], pr...  32.2 us
    reduce_sum x17, other arithmetic, attend_tile(): totals = totals * fading + jnp.sum(probs, axis=-1)  17.7 us
  transfers between devices with their start and end apart: 20, of which 20 were waited for; matrix products, arithmetic and copies ran while one was open for 15% of the time, Pallas kernels for 0%

profile of v1, /device:TPU:1, one launch (start us, length us, event | category | flops | bytes accessed | tf_op | source)
XLA Modules:
  0.0 692.3 jit_solution(11420919164715837436)
XLA Ops:
  11.8 2.5 stack.6
  14.3 8.1 %all-to-all-start = ((bf16[4,128,4096]{2,1,0:T(8,128)(2,1)}), bf16[4,128,4096]{2,1,0:T(8,128)(2,1)}, u32[]{:S(2)}, u32[]{:S(2)}) async-start(bf16[4,128,4096]{2,1,0:T(8,128)(2,1)} %stack.6), calls=%async_computation | async-start | bytes 8388608 | tf_op jit(solution)/shard_map/all_to_all | solution.py:59
  24.5 59.8 %all-to-all-done = bf16[4,128,4096]{2,1,0:T(8,128)(2,1)} async-done(((bf16[4,128,4096]{2,1,0:T(8,128)(2,1)}), bf16[4,128,4096]{2,1,0:T(8,128)(2,1)}, u32[]{:S(2)}, u32[]{:S(2)}) %all-to-all-start) | async-done | bytes 4194336 | tf_op jit(solution)/shard_map/all_to_all | solution.py:59
  84.3 191.5 %all-gather.3.cloned.1.call-done = bf16[4096,768]{1,0:T(8,128)(2,1)} async-done(((bf16[64,768]{1,0:T(8,128)(2,1)}), bf16[4096,768]{1,0:T(8,128)(2,1)}) %all-gather.3.cloned.1.call-update) | async-done | bytes 6291472 | tf_op jit(solution)/shard_map/all_gather | solution.py:15
  275.8 4.2 fusion.27
  280.8 4.4 slice_bitcast_fusion.4
  285.2 6.4 copy.24
  291.6 5.8 fusion.62
  301.6 214.4 %while.22 = (s32[]{:T(128)}, bf16[512,2,1,128]{3,0,2,1:T(8,128)(2,1)S(1)}, f32[1,4,512]{2,1,0:T(4,128)S(1)}, f32[1,4,512]{2,1,0:T(4,128)S(1)}, f32[1,4,512,128]{...) while((s32[]{:T(128)}, ...), condition=%wide.region_10.11_spmd.clone, body=%wide.region_6.10_spmd.clone.sunk | while | flops 552107520 | bytes 18236672 | solution.py:130
  303.5 3.3 collective-permute-done
  310.8 3.8 collective-permute-start
  315.1 2.9 collective-permute-done
  320.1 1.9 fusion.77
  322.0 3.8 collective-permute-start
  326.3 2.8 collective-permute-done
  333.0 3.8 collective-permute-start
  337.3 3.8 collective-permute-done
  345.1 3.8 collective-permute-start
  349.4 7.0 %collective-permute-done = bf16[512,2,1,128]{3,0,2,1:T(8,128)(2,1)S(1)} collective-permute-done((bf16[512,2,1,128]{3,0,2,1:T(8,128)(2,1)S(1)}, bf16[512,2,1,128]{3,0,2,1:T(8,128)(2,1)S(1)}, u32[]{:S(2)}, u32[]{:S(2)}) %collective-permute-start) | collective-permute-done | bytes 262176 | tf_op jit(solution)/shard_map/while/body/eval_jaxpr/ppermute | solution.py:26
  360.3 4.1 collective-permute-start
  364.9 5.2 collective-permute-done
  374.0 4.2 collective-permute-start
  378.7 4.5 collective-permute-done
  387.1 4.3 collective-permute-start
  391.9 4.0 collective-permute-done
  397.9 1.9 fusion.77
  399.8 4.6 collective-permute-start
  404.9 3.2 collective-permute-done
  412.0 8.0 %collective-permute-start = (bf16[512,2,1,128]{3,0,2,1:T(8,128)(2,1)S(1)}, bf16[512,2,1,128]{3,0,2,1:T(8,128)(2,1)S(1)}, u32[]{:S(2)}, u32[]{:S(2)}) collective-permute-start(bf16[512,2,1,128]{3,0,2,1:T(8,128)(2,1)S(1)} %get-tuple-element.419), channel_id=1, source_target_pairs={{0,1},{1,2},{2,3},{3,4},{4,5},{5,6},{6,7},{7,8},{8,9},{9,10},{10,1... | collective-permute-start | bytes 786440 | tf_op jit(solution)/shard_map/while/body/eval_jaxpr/ppermute | solution.py:26
  420.4 5.2 collective-permute-done
  429.5 4.1 collective-permute-start
  434.0 4.2 collective-permute-done
  442.2 4.2 collective-permute-start
  446.9 2.9 collective-permute-done
  451.8 1.9 fusion.77
  453.7 11.6 %collective-permute-start = (bf16[512,2,1,128]{3,0,2,1:T(8,128)(2,1)S(1)}, bf16[512,2,1,128]{3,0,2,1:T(8,128)(2,1)S(1)}, u32[]{:S(2)}, u32[]{:S(2)}) collective-permute-start(bf16[512,2,1,128]{3,0,2,1:T(8,128)(2,1)S(1)} %get-tuple-element.419), channel_id=1, source_target_pairs={{0,1},{1,2},{2,3},{3,4},{4,5},{5,6},{6,7},{7,8},{8,9},{9,10},{10,1... | collective-permute-start | bytes 786440 | tf_op jit(solution)/shard_map/while/body/eval_jaxpr/ppermute | solution.py:26
  465.8 4.6 collective-permute-done
  472.4 1.9 fusion.77
  474.3 5.6 collective-permute-start
  480.4 3.7 collective-permute-done
  488.0 5.5 collective-permute-start
  494.0 3.6 collective-permute-done
  499.6 1.9 fusion.77
  501.5 6.6 collective-permute-start
  508.6 3.3 collective-permute-done
  516.5 61.1 %all-gather.5.cloned.1.call-done = bf16[512,4096]{1,0:T(8,128)(2,1)} async-done(((bf16[8,4096]{1,0:T(8,128)(2,1)}), bf16[512,4096]{1,0:T(8,128)(2,1)}) %all-gather.5.cloned.1.call-update) | async-done | bytes 4194320 | tf_op jit(solution)/shard_map/all_gather | solution.py:134
  577.6 6.5 convolution_convert_fusion
  584.1 101.7 %reduce-scatter.2.cloned.1.call-done = bf16[128,4096]{1,0:T(8,128)(2,1)} async-done(((bf16[512,4096]{1,0:T(8,128)(2,1)}), bf16[128,4096]{1,0:T(8,128)(2,1)}) %reduce-scatter.2.cloned.1.call-update) | async-done | bytes 1048592 | tf_op jit(solution)/shard_map/reduce_scatter | solution.py:135
  (208 shorter events, 73.6 us)
Async XLA Ops:
  6.5 269.3 %all-gather.3.cloned.1.call-start = ((), (), s32[]{:S(2)}) async-start(), calls=%async_computation.2 | async-start | bytes 6389760 | tf_op jit(solution)/shard_map/all_gather | solution.py:15
  14.3 8.9 %copy-start = (s32[16]{0:T(128)S(1)}, s32[16]{0:T(128)}, u32[]{:S(2)}) copy-start(s32[16]{0:T(128)} %param.11) | copy-start | bytes 196
  14.3 70.0 %all-to-all-start = ((bf16[4,128,4096]{2,1,0:T(8,128)(2,1)}), bf16[4,128,4096]{2,1,0:T(8,128)(2,1)}, u32[]{:S(2)}, u32[]{:S(2)}) async-start(bf16[4,128,4096]{2,1,0:T(8,128)(2,1)} %stack.6), calls=%async_computation | async-start | bytes 8388608 | tf_op jit(solution)/shard_map/all_to_all | solution.py:59
  22.5 555.1 %all-gather.5.cloned.1.call-start = ((), (), s32[]{:S(2)}) async-start(), calls=%async_computation.3 | async-start | bytes 4259840 | tf_op jit(solution)/shard_map/all_gather | solution.py:134
  23.2 662.6 %reduce-scatter.2.cloned.1.call-start = ((), (), s32[]{:S(2)}) async-start(), calls=%async_computation.4 | async-start | bytes 5242880 | tf_op jit(solution)/shard_map/reduce_scatter | solution.py:135
  301.6 5.3 collective-permute-start
  310.8 7.3 %collective-permute-start = (bf16[512,2,1,128]{3,0,2,1:T(8,128)(2,1)S(1)}, bf16[512,2,1,128]{3,0,2,1:T(8,128)(2,1)S(1)}, u32[]{:S(2)}, u32[]{:S(2)}) collective-permute-start(bf16[512,2,1,128]{3,0,2,1:T(8,128)(2,1)S(1)} %get-tuple-element.419), channel_id=1, source_target_pairs={{0,1},{1,2},{2,3},{3,4},{4,5},{5,6},{6,7},{7,8},{8,9},{9,10},{10,1... | collective-permute-start | bytes 786440 | tf_op jit(solution)/shard_map/while/body/eval_jaxpr/ppermute | solution.py:26
  322.0 7.1 %collective-permute-start = (bf16[512,2,1,128]{3,0,2,1:T(8,128)(2,1)S(1)}, bf16[512,2,1,128]{3,0,2,1:T(8,128)(2,1)S(1)}, u32[]{:S(2)}, u32[]{:S(2)}) collective-permute-start(bf16[512,2,1,128]{3,0,2,1:T(8,128)(2,1)S(1)} %get-tuple-element.419), channel_id=1, source_target_pairs={{0,1},{1,2},{2,3},{3,4},{4,5},{5,6},{6,7},{7,8},{8,9},{9,10},{10,1... | collective-permute-start | bytes 786440 | tf_op jit(solution)/shard_map/while/body/eval_jaxpr/ppermute | solution.py:26
  333.0 8.1 %collective-permute-start = (bf16[512,2,1,128]{3,0,2,1:T(8,128)(2,1)S(1)}, bf16[512,2,1,128]{3,0,2,1:T(8,128)(2,1)S(1)}, u32[]{:S(2)}, u32[]{:S(2)}) collective-permute-start(bf16[512,2,1,128]{3,0,2,1:T(8,128)(2,1)S(1)} %get-tuple-element.419), channel_id=1, source_target_pairs={{0,1},{1,2},{2,3},{3,4},{4,5},{5,6},{6,7},{7,8},{8,9},{9,10},{10,1... | collective-permute-start | bytes 786440 | tf_op jit(solution)/shard_map/while/body/eval_jaxpr/ppermute | solution.py:26
  345.1 11.3 %collective-permute-start = (bf16[512,2,1,128]{3,0,2,1:T(8,128)(2,1)S(1)}, bf16[512,2,1,128]{3,0,2,1:T(8,128)(2,1)S(1)}, u32[]{:S(2)}, u32[]{:S(2)}) collective-permute-start(bf16[512,2,1,128]{3,0,2,1:T(8,128)(2,1)S(1)} %get-tuple-element.419), channel_id=1, source_target_pairs={{0,1},{1,2},{2,3},{3,4},{4,5},{5,6},{6,7},{7,8},{8,9},{9,10},{10,1... | collective-permute-start | bytes 786440 | tf_op jit(solution)/shard_map/while/body/eval_jaxpr/ppermute | solution.py:26
  360.3 9.8 %collective-permute-start = (bf16[512,2,1,128]{3,0,2,1:T(8,128)(2,1)S(1)}, bf16[512,2,1,128]{3,0,2,1:T(8,128)(2,1)S(1)}, u32[]{:S(2)}, u32[]{:S(2)}) collective-permute-start(bf16[512,2,1,128]{3,0,2,1:T(8,128)(2,1)S(1)} %get-tuple-element.419), channel_id=1, source_target_pairs={{0,1},{1,2},{2,3},{3,4},{4,5},{5,6},{6,7},{7,8},{8,9},{9,10},{10,1... | collective-permute-start | bytes 786440 | tf_op jit(solution)/shard_map/while/body/eval_jaxpr/ppermute | solution.py:26
  374.0 9.2 %collective-permute-start = (bf16[512,2,1,128]{3,0,2,1:T(8,128)(2,1)S(1)}, bf16[512,2,1,128]{3,0,2,1:T(8,128)(2,1)S(1)}, u32[]{:S(2)}, u32[]{:S(2)}) collective-permute-start(bf16[512,2,1,128]{3,0,2,1:T(8,128)(2,1)S(1)} %get-tuple-element.419), channel_id=1, source_target_pairs={{0,1},{1,2},{2,3},{3,4},{4,5},{5,6},{6,7},{7,8},{8,9},{9,10},{10,1... | collective-permute-start | bytes 786440 | tf_op jit(solution)/shard_map/while/body/eval_jaxpr/ppermute | solution.py:26
  387.1 8.8 %collective-permute-start = (bf16[512,2,1,128]{3,0,2,1:T(8,128)(2,1)S(1)}, bf16[512,2,1,128]{3,0,2,1:T(8,128)(2,1)S(1)}, u32[]{:S(2)}, u32[]{:S(2)}) collective-permute-start(bf16[512,2,1,128]{3,0,2,1:T(8,128)(2,1)S(1)} %get-tuple-element.419), channel_id=1, source_target_pairs={{0,1},{1,2},{2,3},{3,4},{4,5},{5,6},{6,7},{7,8},{8,9},{9,10},{10,1... | collective-permute-start | bytes 786440 | tf_op jit(solution)/shard_map/while/body/eval_jaxpr/ppermute | solution.py:26
  399.8 8.2 %collective-permute-start = (bf16[512,2,1,128]{3,0,2,1:T(8,128)(2,1)S(1)}, bf16[512,2,1,128]{3,0,2,1:T(8,128)(2,1)S(1)}, u32[]{:S(2)}, u32[]{:S(2)}) collective-permute-start(bf16[512,2,1,128]{3,0,2,1:T(8,128)(2,1)S(1)} %get-tuple-element.419), channel_id=1, source_target_pairs={{0,1},{1,2},{2,3},{3,4},{4,5},{5,6},{6,7},{7,8},{8,9},{9,10},{10,1... | collective-permute-start | bytes 786440 | tf_op jit(solution)/shard_map/while/body/eval_jaxpr/ppermute | solution.py:26
  412.0 13.6 %collective-permute-start = (bf16[512,2,1,128]{3,0,2,1:T(8,128)(2,1)S(1)}, bf16[512,2,1,128]{3,0,2,1:T(8,128)(2,1)S(1)}, u32[]{:S(2)}, u32[]{:S(2)}) collective-permute-start(bf16[512,2,1,128]{3,0,2,1:T(8,128)(2,1)S(1)} %get-tuple-element.419), channel_id=1, source_target_pairs={{0,1},{1,2},{2,3},{3,4},{4,5},{5,6},{6,7},{7,8},{8,9},{9,10},{10,1... | collective-permute-start | bytes 786440 | tf_op jit(solution)/shard_map/while/body/eval_jaxpr/ppermute | solution.py:26
  429.5 8.8 %collective-permute-start = (bf16[512,2,1,128]{3,0,2,1:T(8,128)(2,1)S(1)}, bf16[512,2,1,128]{3,0,2,1:T(8,128)(2,1)S(1)}, u32[]{:S(2)}, u32[]{:S(2)}) collective-permute-start(bf16[512,2,1,128]{3,0,2,1:T(8,128)(2,1)S(1)} %get-tuple-element.419), channel_id=1, source_target_pairs={{0,1},{1,2},{2,3},{3,4},{4,5},{5,6},{6,7},{7,8},{8,9},{9,10},{10,1... | collective-permute-start | bytes 786440 | tf_op jit(solution)/shard_map/while/body/eval_jaxpr/ppermute | solution.py:26
  442.2 7.6 %collective-permute-start = (bf16[512,2,1,128]{3,0,2,1:T(8,128)(2,1)S(1)}, bf16[512,2,1,128]{3,0,2,1:T(8,128)(2,1)S(1)}, u32[]{:S(2)}, u32[]{:S(2)}) collective-permute-start(bf16[512,2,1,128]{3,0,2,1:T(8,128)(2,1)S(1)} %get-tuple-element.419), channel_id=1, source_target_pairs={{0,1},{1,2},{2,3},{3,4},{4,5},{5,6},{6,7},{7,8},{8,9},{9,10},{10,1... | collective-permute-start | bytes 786440 | tf_op jit(solution)/shard_map/while/body/eval_jaxpr/ppermute | solution.py:26
  453.7 16.6 %collective-permute-start = (bf16[512,2,1,128]{3,0,2,1:T(8,128)(2,1)S(1)}, bf16[512,2,1,128]{3,0,2,1:T(8,128)(2,1)S(1)}, u32[]{:S(2)}, u32[]{:S(2)}) collective-permute-start(bf16[512,2,1,128]{3,0,2,1:T(8,128)(2,1)S(1)} %get-tuple-element.419), channel_id=1, source_target_pairs={{0,1},{1,2},{2,3},{3,4},{4,5},{5,6},{6,7},{7,8},{8,9},{9,10},{10,1... | collective-permute-start | bytes 786440 | tf_op jit(solution)/shard_map/while/body/eval_jaxpr/ppermute | solution.py:26
  474.3 9.8 %collective-permute-start = (bf16[512,2,1,128]{3,0,2,1:T(8,128)(2,1)S(1)}, bf16[512,2,1,128]{3,0,2,1:T(8,128)(2,1)S(1)}, u32[]{:S(2)}, u32[]{:S(2)}) collective-permute-start(bf16[512,2,1,128]{3,0,2,1:T(8,128)(2,1)S(1)} %get-tuple-element.419), channel_id=1, source_target_pairs={{0,1},{1,2},{2,3},{3,4},{4,5},{5,6},{6,7},{7,8},{8,9},{9,10},{10,1... | collective-permute-start | bytes 786440 | tf_op jit(solution)/shard_map/while/body/eval_jaxpr/ppermute | solution.py:26
  488.0 9.6 %collective-permute-start = (bf16[512,2,1,128]{3,0,2,1:T(8,128)(2,1)S(1)}, bf16[512,2,1,128]{3,0,2,1:T(8,128)(2,1)S(1)}, u32[]{:S(2)}, u32[]{:S(2)}) collective-permute-start(bf16[512,2,1,128]{3,0,2,1:T(8,128)(2,1)S(1)} %get-tuple-element.419), channel_id=1, source_target_pairs={{0,1},{1,2},{2,3},{3,4},{4,5},{5,6},{6,7},{7,8},{8,9},{9,10},{10,1... | collective-permute-start | bytes 786440 | tf_op jit(solution)/shard_map/while/body/eval_jaxpr/ppermute | solution.py:26
  501.5 10.4 %collective-permute-start = (bf16[512,2,1,128]{3,0,2,1:T(8,128)(2,1)S(1)}, bf16[512,2,1,128]{3,0,2,1:T(8,128)(2,1)S(1)}, u32[]{:S(2)}, u32[]{:S(2)}) collective-permute-start(bf16[512,2,1,128]{3,0,2,1:T(8,128)(2,1)S(1)} %get-tuple-element.419), channel_id=1, source_target_pairs={{0,1},{1,2},{2,3},{3,4},{4,5},{5,6},{6,7},{7,8},{8,9},{9,10},{10,1... | collective-permute-start | bytes 786440 | tf_op jit(solution)/shard_map/while/body/eval_jaxpr/ppermute | solution.py:26
Sparse Core Ops, SparseCore 0:
  9.1 266.6 all-gather.2
  277.6 299.9 all-gather.4
  584.2 101.5 reduce-scatter.1
